TPU v7x, 32 devices: a whole 2x2x4 slice. The times are simulated.
32 devices in a mesh: section: 4 (over y, core), sim: 8 (over z, x).
Axes of the slice: x: 2, y: 2, z: 4, core: 2. Of those that a mesh axis runs over, the one named last changes fastest.
Arguments:
- state: float32 [128, 64, 8192], P('section', None, 'sim'), may hold values from -60 to 60
- owner: int32 [128, 1], P('section'), may hold values from 0 to 7; in each aligned block of 32 rows (0 to 31, 32 to 63, ...) at most 8 rows name the same one
- counts: int32 [128], P('section'), may hold values from 2048 to 8192
Outputs:
- slab_mean: float32 [128, 64], P('section')
- slab_cov: float32 [128, 4096], P('section', 'sim')
- group_cov: float32 [32, 4096], P(('section', 'sim'))
- global_mean: float32 [64], replicated
- global_cov: float32 [64, 64], replicated
Inputs may be any that keep to these rules, and one draw needn't show every extreme that they name: Among the 32 slabs of one group, no owner is named by more than 8 slabs, and one owner is named by exactly 8 slabs in some or all groups.
All inputs are finite; a program needn't handle non-finite values.
Results may differ from a plain program's by a relative error of at most 0.0003.
Values sent between devices are 32-bit elements; how exact they have to be, the bound alone decides.
A program may use at most 64 MiB of HBM per device.

v0:
```python
import jax
import jax.numpy as jnp
from jax import lax
from jax.sharding import PartitionSpec as P


def slot_payload(number, mean, comoment, capacity, n_sim, width):
    slot_cov = comoment / jnp.maximum(number - 1.0, 1.0)[:, None]
    cov_parts = slot_cov.reshape(capacity, n_sim, width * width // n_sim)
    mean_copies = jnp.broadcast_to(mean[:, None, :], (capacity, n_sim, width))
    return (cov_parts, mean_copies)


def owner_stats(number, mean, comoment):
    high = lax.Precision.HIGHEST
    width = mean.shape[1]
    group_count = jnp.sum(number)
    group_mean = jnp.sum(number[:, None] * mean, axis=0) / jnp.maximum(group_count, 1.0)
    offset = mean - group_mean[None, :]
    group_co = jnp.sum(comoment, axis=0) + jnp.einsum(
        "k,kv,kw->vw", number, offset, offset, precision=high
    ).reshape(width * width)
    return (group_count, group_mean, group_co)


def local(state, owner, counts):
    high = lax.Precision.HIGHEST
    slab_here, width, cells_dev = state.shape
    n_sim = lax.axis_size("sim")
    my_index = lax.axis_index("sim")
    capacity = 2 * slab_here // n_sim
    slots = n_sim * capacity
    target = owner[:, 0]
    order = jnp.arange(slab_here, dtype=jnp.int32)
    earlier = (target[:, None] == target[None, :]) & (order[None, :] < order[:, None])
    rank = jnp.sum(earlier.astype(jnp.int32), axis=1)
    slot_of = target * capacity + rank
    match = slot_of[:, None] == jnp.arange(slots, dtype=jnp.int32)[None, :]
    filled = jnp.any(match, axis=0)
    source_slab = jnp.sum(jnp.where(match, order[:, None], 0), axis=0)
    tile_start = my_index * cells_dev
    tile_count = jnp.clip(counts - tile_start, 0, cells_dev).astype(jnp.float32)
    live = jnp.arange(cells_dev, dtype=jnp.int32)[None, :] + tile_start < counts[:, None]
    tile_mean = (
        jnp.sum(jnp.where(live[:, None, :], state, 0.0), axis=2)
        / jnp.maximum(tile_count, 1.0)[:, None]
    )
    centered = jnp.where(live[:, None, :], state - tile_mean[:, :, None], 0.0)
    tile_co = jnp.einsum("svc,swc->svw", centered, centered, precision=high).reshape(
        slab_here, width * width
    )
    send_mean = jnp.where(filled[:, None], tile_mean[source_slab], 0.0).reshape(
        n_sim, capacity, width
    )
    send_co = jnp.where(filled[:, None], tile_co[source_slab], 0.0).reshape(
        n_sim, capacity, width * width
    )
    send_count = jnp.where(filled, tile_count[source_slab], 0.0).reshape(n_sim, capacity)
    means = lax.all_to_all(send_mean, "sim", split_axis=0, concat_axis=0, tiled=True)
    comoms = lax.all_to_all(send_co, "sim", split_axis=0, concat_axis=0, tiled=True)
    amounts = lax.all_to_all(send_count, "sim", split_axis=0, concat_axis=0, tiled=True)
    number = jnp.sum(amounts, axis=0)
    mean = jnp.sum(amounts[:, :, None] * means, axis=0) / jnp.maximum(number, 1.0)[:, None]
    offset = means - mean[None, :, :]
    extra = jnp.einsum("ik,ikv,ikw->kvw", amounts, offset, offset, precision=high)
    number, mean, comoment = (
        number,
        mean,
        jnp.sum(comoms, axis=0) + extra.reshape(number.shape[0], width * width),
    )
    cov_parts, mean_copies = slot_payload(number, mean, comoment, capacity, n_sim, width)
    back_cov, back_mean = (
        lax.all_to_all(cov_parts, "sim", split_axis=1, concat_axis=0, tiled=True),
        lax.all_to_all(mean_copies, "sim", split_axis=1, concat_axis=0, tiled=True),
    )
    slab_cov = back_cov[slot_of, 0]
    slab_mean = back_mean[slot_of, 0]
    group_count, group_mean, group_co = owner_stats(number, mean, comoment)
    group_cov = (group_co / jnp.maximum(group_count - 1.0, 1.0))[None, :]
    total, weighted = lax.psum((group_count, group_count * group_mean), ("section", "sim"))
    global_mean = weighted / total
    gap = group_mean - global_mean
    spread = lax.psum(group_co + group_count * jnp.outer(gap, gap).reshape(-1), ("section", "sim"))
    global_cov = (spread / (total - 1.0)).reshape(width, width)
    return (slab_mean, slab_cov, group_cov, global_mean, global_cov)


def solution(mesh):
    return jax.shard_map(
        local,
        mesh=mesh,
        in_specs=(P("section", None, "sim"), P("section", None), P("section")),
        out_specs=(P("section", None), P("section", "sim"), P(("section", "sim"), None), P(), P()),
        check_vma=False,
    )
```

profile of v0, /device:TPU:0, one launch (start us, length us, event | category | flops | bytes accessed | tf_op | source)
XLA Modules:
  0.0 160.8 jit_solution(15916009984353185825)
XLA Ops:
  0.6 0.9 convert_reduce_fusion
  1.5 0.7 fusion.19
  2.2 0.1 fusion.10
  2.3 0.1 select_reduce_fusion.1
  2.4 0.7 broadcast_maximum_fusion.1
  3.1 0.8 gather_fusion
  3.9 0.7 select_n.56
  4.5 7.3 %all-to-all-start = ((f32[8,1,8]{2,1,0:T(1,128)}), f32[8,1,8]{2,1,0:T(1,128)S(1)}, u32[]{:S(2)}, u32[]{:S(2)}) async-start(f32[8,1,8]{2,1,0:T(1,128)} %bitcast.5), calls=%async_computation | async-start | bytes 8192 | tf_op jit(solution)/shard_map/all_to_all | solution.py:61
  11.8 0.1 broadcast_in_dim.63
  11.9 0.7 broadcast_compare_fusion
  12.7 4.1 %select_reduce_fusion = f32[32,64]{1,0:T(8,128)S(1)} fusion(f32[32,64,1024]{2,1,0:T(8,128)} %param.3, pred[32,1024]{1,0:T(8,128)(4,1)S(1)} %broadcast_compare_fusion), kind=kLoop, calls=%fused_computation.8 | loop fusion | flops 4192256 | bytes 8429568 | tf_op jit(solution)/shard_map/reduce_sum | solution.py:45
  16.8 0.1 broadcast_divide_fusion.2
  16.9 0.6 gather_fusion.1
  17.5 14.9 %fusion = f32[32,64,64]{2,1,0:T(8,128)S(1)} fusion(f32[32,64,1024]{2,1,0:T(8,128)} %param.3, f32[32,64]{1,0:T(8,128)S(1)} %broadcast_divide_fusion.2, pred[32,1024]{1,0:T(8,128)(4,1)S(1)} %broadcast_compare_fusion), kind=kOutput, calls=%fused_computation.5 | convolution fusion | flops 1614807040 | bytes 8953856 | tf_op jit(solution)/shard_map/svc,swc->svw/dot_general | solution.py:49
  32.4 0.1 bitcast_select_fusion.1
  32.5 0.7 reshape.244
  33.2 0.4 reshape.205
  33.5 0.9 gather_fusion.3
  34.5 0.0 all-to-all-done
  34.5 6.0 %all-to-all-start.1 = ((f32[8,1,512]{2,1,0:T(1,128)}), f32[8,1,512]{2,1,0:T(1,128)S(1)}, u32[]{:S(2)}, u32[]{:S(2)}) async-start(f32[8,1,512]{2,1,0:T(1,128)} %reshape.244), calls=%async_computation.1 | async-start | bytes 32768 | tf_op jit(solution)/shard_map/all_to_all | solution.py:59
  40.5 0.6 fusion.22
  41.1 6.0 %all-to-all-done.1 = f32[8,1,512]{2,1,0:T(1,128)S(1)} async-done(((f32[8,1,512]{2,1,0:T(1,128)}), f32[8,1,512]{2,1,0:T(1,128)S(1)}, u32[]{:S(2)}, u32[]{:S(2)}) %all-to-all-start.1) | async-done | bytes 16416 | tf_op jit(solution)/shard_map/all_to_all | solution.py:59
  47.1 0.5 broadcast.202
  47.6 0.7 reduce.4
  48.3 0.1 reshape.245
  48.3 0.1 multiply_reduce_fusion
  48.4 0.1 multiply_reduce_fusion.1
  48.5 0.7 reshape.246
  49.2 3.3 %all-to-all-start.2 = ((f32[8,1,512]{2,1,0:T(1,128)}), f32[8,1,512]{2,1,0:T(1,128)S(1)}, u32[]{:S(2)}, u32[]{:S(2)}) async-start(f32[8,1,512]{2,1,0:T(1,128)} %reshape.246), calls=%async_computation.2 | async-start | bytes 32768 | tf_op jit(solution)/shard_map/all_to_all | solution.py:74
  52.6 1.1 bitcast_select_fusion
  53.7 5.4 %all-to-all-done.2 = f32[8,1,512]{2,1,0:T(1,128)S(1)} async-done(((f32[8,1,512]{2,1,0:T(1,128)}), f32[8,1,512]{2,1,0:T(1,128)S(1)}, u32[]{:S(2)}, u32[]{:S(2)}) %all-to-all-start.2) | async-done | bytes 16416 | tf_op jit(solution)/shard_map/all_to_all | solution.py:74
  59.1 3.6 %all-to-all-start.3 = ((f32[8,8,4096]{2,1,0:T(8,128)}), f32[8,8,4096]{2,1,0:T(8,128)S(1)}, u32[]{:S(2)}, u32[]{:S(2)}) async-start(f32[8,8,4096]{2,1,0:T(8,128)} %bitcast_select_fusion), calls=%async_computation.3 | async-start | bytes 2097152 | tf_op jit(solution)/shard_map/all_to_all | solution.py:60
  63.9 0.7 broadcast_multiply_fusion.1
  64.6 41.6 %all-reduce.1 = (f32[64]{0:T(128)S(1)}, f32[]{:T(128)}) all-reduce(f32[64]{0:T(128)S(1)} %get-tuple-element.11, f32[]{:T(128)} %get-tuple-element.5), channel_id=1, replica_groups=mesh['section'=4,'sim'=8] {'section','sim'}, use_global_device_ids=true, to_apply=%region_10.11 | all-reduce | flops 65 | bytes 520 | tf_op jit(solution)/shard_map/psum | solution.py:80
  106.8 1.2 fusion.23
  108.0 0.1 broadcast_multiply_fusion
  108.1 0.7 reduce.5
  108.8 0.1 reshape.247
  108.8 1.2 gather_fusion.2
  110.0 0.0 all-to-all-done.3
  110.0 0.1 reduce_sum.96
  110.1 0.1 reduce_sum.98
  110.2 0.6 add_reduce_fusion
  110.8 0.1 reshape.206
  110.9 0.7 fusion.6
  111.7 5.3 %all-to-all-start.4 = ((f32[8,8,512]{2,0,1:T(8,128)}), f32[8,8,512]{2,0,1:T(8,128)S(1)}, u32[]{:S(2)}, u32[]{:S(2)}) async-start(f32[8,8,512]{2,0,1:T(8,128)} %fusion.6), calls=%async_computation.4 | async-start | bytes 262144 | tf_op jit(solution)/shard_map/all_to_all | solution.py:73
  117.0 1.0 multiply_add_fusion
  117.9 0.7 div.85
  118.6 0.1 add.82
  118.7 40.0 %psum.23 = f32[4096]{0:T(1024)S(1)} all-reduce(f32[4096]{0:T(1024)S(1)} %add.82), channel_id=1, replica_groups=mesh['section'=4,'sim'=8] {'section','sim'}, use_global_device_ids=true, to_apply=%region_12.13 | all-reduce | flops 4096 | bytes 32768 | tf_op jit(solution)/shard_map/psum | solution.py:83
  158.7 0.7 reshape.207
  159.4 0.0 all-to-all-done.4
  159.4 0.1 all_to_all.46
  159.6 1.2 gather_fusion.4
  (7 shorter events, 0.0 us)
Async XLA Ops:
  4.5 29.9 %all-to-all-start = ((f32[8,1,8]{2,1,0:T(1,128)}), f32[8,1,8]{2,1,0:T(1,128)S(1)}, u32[]{:S(2)}, u32[]{:S(2)}) async-start(f32[8,1,8]{2,1,0:T(1,128)} %bitcast.5), calls=%async_computation | async-start | bytes 8192 | tf_op jit(solution)/shard_map/all_to_all | solution.py:61
  34.5 12.6 %all-to-all-start.1 = ((f32[8,1,512]{2,1,0:T(1,128)}), f32[8,1,512]{2,1,0:T(1,128)S(1)}, u32[]{:S(2)}, u32[]{:S(2)}) async-start(f32[8,1,512]{2,1,0:T(1,128)} %reshape.244), calls=%async_computation.1 | async-start | bytes 32768 | tf_op jit(solution)/shard_map/all_to_all | solution.py:59
  49.2 9.9 %all-to-all-start.2 = ((f32[8,1,512]{2,1,0:T(1,128)}), f32[8,1,512]{2,1,0:T(1,128)S(1)}, u32[]{:S(2)}, u32[]{:S(2)}) async-start(f32[8,1,512]{2,1,0:T(1,128)} %reshape.246), calls=%async_computation.2 | async-start | bytes 32768 | tf_op jit(solution)/shard_map/all_to_all | solution.py:74
  59.1 51.0 %all-to-all-start.3 = ((f32[8,8,4096]{2,1,0:T(8,128)}), f32[8,8,4096]{2,1,0:T(8,128)S(1)}, u32[]{:S(2)}, u32[]{:S(2)}) async-start(f32[8,8,4096]{2,1,0:T(8,128)} %bitcast_select_fusion), calls=%async_computation.3 | async-start | bytes 2097152 | tf_op jit(solution)/shard_map/all_to_all | solution.py:60
  111.7 47.8 %all-to-all-start.4 = ((f32[8,8,512]{2,0,1:T(8,128)}), f32[8,8,512]{2,0,1:T(8,128)S(1)}, u32[]{:S(2)}, u32[]{:S(2)}) async-start(f32[8,8,512]{2,0,1:T(8,128)} %fusion.6), calls=%async_computation.4 | async-start | bytes 262144 | tf_op jit(solution)/shard_map/all_to_all | solution.py:73
where the time goes:
time: 162 us; the launch traced here: 161 us
  blocking collectives  81.6 us (50%)
  starting transfers between devices  25.5 us (16%)
  matrix products  16.5 us (10%)
  other arithmetic  13.4 us (8%)
  waiting for transfers between devices  11.3 us (7%)
  local copies, waits for them, and re-layouts  9.73 us (6%)
  between operations  2.71 us (2%)
    psum x1, blocking collectives, local(): lax.psum((group_count, group_count * group_mean), ('section', 'sim'))  41.6 us
    psum x1, blocking collectives, local(): lax.psum(group_co + group_count * jnp.outer(gap, gap).reshape(-1), ('sect...  40 us
    dot_general x1, matrix products, local(): jnp.einsum('svc,swc->svw', centered, centered, precision=high)  14.9 us
    all_to_all x1, starting transfers between devices, local(): lax.all_to_all(send_count, 'sim', split_axis=0, concat_axis=0, tiled=True)  7.28 us
    all_to_all x1, starting transfers between devices, local(): lax.all_to_all(send_mean, 'sim', split_axis=0, concat_axis=0, tiled=True)  6.01 us
    all_to_all x1, waiting for transfers between devices, local(): lax.all_to_all(send_mean, 'sim', split_axis=0, concat_axis=0, tiled=True)  5.96 us
    all_to_all x1, waiting for transfers between devices, local(): lax.all_to_all(mean_copies, 'sim', split_axis=1, concat_axis=0, tiled=True)  5.37 us
    all_to_all x1, starting transfers between devices, local(): lax.all_to_all(cov_parts, 'sim', split_axis=1, concat_axis=0, tiled=True)  5.31 us
  transfers between devices with their start and end apart: 5, of which 2 were waited for; matrix products, arithmetic and copies ran while one was open for 19% of the time, Pallas kernels for 0%

commit v1 on v0

--- a/solution.py
+++ b/solution.py
@@ -80,7 +80,9 @@
     total, weighted = lax.psum((group_count, group_count * group_mean), ("section", "sim"))
     global_mean = weighted / total
     gap = group_mean - global_mean
-    spread = lax.psum(group_co + group_count * jnp.outer(gap, gap).reshape(-1), ("section", "sim"))
+    spread = group_co + group_count * jnp.outer(gap, gap).reshape(-1)
+    for over in ("section", "sim"):
+        spread = lax.psum(spread, over)
     global_cov = (spread / (total - 1.0)).reshape(width, width)
     return (slab_mean, slab_cov, group_cov, global_mean, global_cov)
 

time: 162 us -> 170 us (1.049)
  blocking collectives: 81.6 us -> 89.6 us
    psum x1 -> x2, blocking collectives: 40 us -> 48 us  [local(): spread = lax.psum(spread, over)]
  transfers between devices with their start and end apart: 5 -> 5, of which waited for: 2 -> 2; matrix products, arithmetic and copies ran while one was open for 19% -> 18% of each run, Pallas kernels for 0% -> 0%
where the time goes in v1:
time: 170 us; the launch traced here: 169 us
  blocking collectives  89.6 us (53%)
  starting transfers between devices  25.5 us (15%)
  matrix products  16.5 us (10%)
  other arithmetic  13.4 us (8%)
  waiting for transfers between devices  11.3 us (7%)
  local copies, waits for them, and re-layouts  9.73 us (6%)
  between operations  2.71 us (2%)
    psum x2, blocking collectives, local(): spread = lax.psum(spread, over)  48 us
    psum x1, blocking collectives, local(): lax.psum((group_count, group_count * group_mean), ('section', 'sim'))  41.6 us
    dot_general x1, matrix products, local(): jnp.einsum('svc,swc->svw', centered, centered, precision=high)  14.9 us
    all_to_all x1, starting transfers between devices, local(): lax.all_to_all(send_count, 'sim', split_axis=0, concat_axis=0, tiled=True)  7.28 us
    all_to_all x1, starting transfers between devices, local(): lax.all_to_all(send_mean, 'sim', split_axis=0, concat_axis=0, tiled=True)  6.01 us
    all_to_all x1, waiting for transfers between devices, local(): lax.all_to_all(send_mean, 'sim', split_axis=0, concat_axis=0, tiled=True)  5.96 us
    all_to_all x1, waiting for transfers between devices, local(): lax.all_to_all(mean_copies, 'sim', split_axis=1, concat_axis=0, tiled=True)  5.37 us
    all_to_all x1, starting transfers between devices, local(): lax.all_to_all(cov_parts, 'sim', split_axis=1, concat_axis=0, tiled=True)  5.31 us
  transfers between devices with their start and end apart: 5, of which 2 were waited for; matrix products, arithmetic and copies ran while one was open for 18% of the time, Pallas kernels for 0%

profile of v1, /device:TPU:0, one launch (start us, length us, event | category | flops | bytes accessed | tf_op | source)
XLA Modules:
  0.0 168.8 jit_solution(5625787766369307550)
XLA Ops:
  0.6 0.9 convert_reduce_fusion
  1.5 0.7 fusion.19
  2.2 0.1 fusion.10
  2.3 0.1 select_reduce_fusion.1
  2.4 0.7 broadcast_maximum_fusion.1
  3.1 0.8 gather_fusion
  3.9 0.7 select_n.56
  4.5 7.3 %all-to-all-start = ((f32[8,1,8]{2,1,0:T(1,128)}), f32[8,1,8]{2,1,0:T(1,128)S(1)}, u32[]{:S(2)}, u32[]{:S(2)}) async-start(f32[8,1,8]{2,1,0:T(1,128)} %bitcast.5), calls=%async_computation | async-start | bytes 8192 | tf_op jit(solution)/shard_map/all_to_all | solution.py:61
  11.8 0.1 broadcast_in_dim.63
  11.9 0.7 broadcast_compare_fusion
  12.7 4.1 %select_reduce_fusion = f32[32,64]{1,0:T(8,128)S(1)} fusion(f32[32,64,1024]{2,1,0:T(8,128)} %param.3, pred[32,1024]{1,0:T(8,128)(4,1)S(1)} %broadcast_compare_fusion), kind=kLoop, calls=%fused_computation.8 | loop fusion | flops 4192256 | bytes 8429568 | tf_op jit(solution)/shard_map/reduce_sum | solution.py:45
  16.8 0.1 broadcast_divide_fusion.2
  16.9 0.6 gather_fusion.1
  17.5 14.9 %fusion = f32[32,64,64]{2,1,0:T(8,128)S(1)} fusion(f32[32,64,1024]{2,1,0:T(8,128)} %param.3, f32[32,64]{1,0:T(8,128)S(1)} %broadcast_divide_fusion.2, pred[32,1024]{1,0:T(8,128)(4,1)S(1)} %broadcast_compare_fusion), kind=kOutput, calls=%fused_computation.5 | convolution fusion | flops 1614807040 | bytes 8953856 | tf_op jit(solution)/shard_map/svc,swc->svw/dot_general | solution.py:49
  32.4 0.1 bitcast_select_fusion.1
  32.5 0.7 reshape.244
  33.2 0.4 reshape.205
  33.5 0.9 gather_fusion.3
  34.5 0.0 all-to-all-done
  34.5 6.0 %all-to-all-start.1 = ((f32[8,1,512]{2,1,0:T(1,128)}), f32[8,1,512]{2,1,0:T(1,128)S(1)}, u32[]{:S(2)}, u32[]{:S(2)}) async-start(f32[8,1,512]{2,1,0:T(1,128)} %reshape.244), calls=%async_computation.1 | async-start | bytes 32768 | tf_op jit(solution)/shard_map/all_to_all | solution.py:59
  40.5 0.6 fusion.22
  41.1 6.0 %all-to-all-done.1 = f32[8,1,512]{2,1,0:T(1,128)S(1)} async-done(((f32[8,1,512]{2,1,0:T(1,128)}), f32[8,1,512]{2,1,0:T(1,128)S(1)}, u32[]{:S(2)}, u32[]{:S(2)}) %all-to-all-start.1) | async-done | bytes 16416 | tf_op jit(solution)/shard_map/all_to_all | solution.py:59
  47.1 0.5 broadcast.202
  47.6 0.7 reduce.4
  48.3 0.1 reshape.245
  48.3 0.1 multiply_reduce_fusion
  48.4 0.1 multiply_reduce_fusion.1
  48.5 0.7 reshape.246
  49.2 3.3 %all-to-all-start.2 = ((f32[8,1,512]{2,1,0:T(1,128)}), f32[8,1,512]{2,1,0:T(1,128)S(1)}, u32[]{:S(2)}, u32[]{:S(2)}) async-start(f32[8,1,512]{2,1,0:T(1,128)} %reshape.246), calls=%async_computation.2 | async-start | bytes 32768 | tf_op jit(solution)/shard_map/all_to_all | solution.py:74
  52.6 1.1 bitcast_select_fusion
  53.7 5.4 %all-to-all-done.2 = f32[8,1,512]{2,1,0:T(1,128)S(1)} async-done(((f32[8,1,512]{2,1,0:T(1,128)}), f32[8,1,512]{2,1,0:T(1,128)S(1)}, u32[]{:S(2)}, u32[]{:S(2)}) %all-to-all-start.2) | async-done | bytes 16416 | tf_op jit(solution)/shard_map/all_to_all | solution.py:74
  59.1 3.6 %all-to-all-start.3 = ((f32[8,8,4096]{2,1,0:T(8,128)}), f32[8,8,4096]{2,1,0:T(8,128)S(1)}, u32[]{:S(2)}, u32[]{:S(2)}) async-start(f32[8,8,4096]{2,1,0:T(8,128)} %bitcast_select_fusion), calls=%async_computation.3 | async-start | bytes 2097152 | tf_op jit(solution)/shard_map/all_to_all | solution.py:60
  63.9 0.7 broadcast_multiply_fusion.1
  64.6 41.6 %all-reduce.1 = (f32[64]{0:T(128)S(1)}, f32[]{:T(128)}) all-reduce(f32[64]{0:T(128)S(1)} %get-tuple-element.11, f32[]{:T(128)} %get-tuple-element.5), channel_id=1, replica_groups=mesh['section'=4,'sim'=8] {'section','sim'}, use_global_device_ids=true, to_apply=%region_10.11 | all-reduce | flops 65 | bytes 520 | tf_op jit(solution)/shard_map/psum | solution.py:80
  106.8 1.2 fusion.23
  108.0 0.1 broadcast_multiply_fusion
  108.1 0.7 reduce.5
  108.8 0.1 reshape.247
  108.8 1.2 gather_fusion.2
  110.0 0.0 all-to-all-done.3
  110.0 0.1 reduce_sum.96
  110.1 0.1 reduce_sum.98
  110.2 0.6 add_reduce_fusion
  110.8 0.1 reshape.206
  110.9 0.7 fusion.6
  111.7 5.3 %all-to-all-start.4 = ((f32[8,8,512]{2,0,1:T(8,128)}), f32[8,8,512]{2,0,1:T(8,128)S(1)}, u32[]{:S(2)}, u32[]{:S(2)}) async-start(f32[8,8,512]{2,0,1:T(8,128)} %fusion.6), calls=%async_computation.4 | async-start | bytes 262144 | tf_op jit(solution)/shard_map/all_to_all | solution.py:73
  117.0 1.0 multiply_add_fusion
  117.9 0.7 div.85
  118.6 0.1 add.84
  118.7 10.4 %psum.30 = f32[4096]{0:T(1024)S(1)} all-reduce(f32[4096]{0:T(1024)S(1)} %add.84), channel_id=1, replica_groups=mesh['section'=4,'sim'=8] {'section'}, use_global_device_ids=true, to_apply=%region_12.13 | all-reduce | flops 4096 | bytes 32768 | tf_op jit(solution)/shard_map/psum | solution.py:85
  129.1 37.6 %psum.31 = f32[4096]{0:T(1024)S(1)} all-reduce(f32[4096]{0:T(1024)S(1)} %psum.30), channel_id=1, replica_groups=mesh['section'=4,'sim'=8] {'sim'}, use_global_device_ids=true, to_apply=%region_13.14 | all-reduce | flops 4096 | bytes 32768 | tf_op jit(solution)/shard_map/psum | solution.py:85
  166.7 0.7 reshape.207
  167.4 0.0 all-to-all-done.4
  167.4 0.1 all_to_all.46
  167.5 1.2 gather_fusion.4
  (7 shorter events, 0.0 us)
Async XLA Ops:
  4.5 29.9 %all-to-all-start = ((f32[8,1,8]{2,1,0:T(1,128)}), f32[8,1,8]{2,1,0:T(1,128)S(1)}, u32[]{:S(2)}, u32[]{:S(2)}) async-start(f32[8,1,8]{2,1,0:T(1,128)} %bitcast.5), calls=%async_computation | async-start | bytes 8192 | tf_op jit(solution)/shard_map/all_to_all | solution.py:61
  34.5 12.6 %all-to-all-start.1 = ((f32[8,1,512]{2,1,0:T(1,128)}), f32[8,1,512]{2,1,0:T(1,128)S(1)}, u32[]{:S(2)}, u32[]{:S(2)}) async-start(f32[8,1,512]{2,1,0:T(1,128)} %reshape.244), calls=%async_computation.1 | async-start | bytes 32768 | tf_op jit(solution)/shard_map/all_to_all | solution.py:59
  49.2 9.9 %all-to-all-start.2 = ((f32[8,1,512]{2,1,0:T(1,128)}), f32[8,1,512]{2,1,0:T(1,128)S(1)}, u32[]{:S(2)}, u32[]{:S(2)}) async-start(f32[8,1,512]{2,1,0:T(1,128)} %reshape.246), calls=%async_computation.2 | async-start | bytes 32768 | tf_op jit(solution)/shard_map/all_to_all | solution.py:74
  59.1 51.0 %all-to-all-start.3 = ((f32[8,8,4096]{2,1,0:T(8,128)}), f32[8,8,4096]{2,1,0:T(8,128)S(1)}, u32[]{:S(2)}, u32[]{:S(2)}) async-start(f32[8,8,4096]{2,1,0:T(8,128)} %bitcast_select_fusion), calls=%async_computation.3 | async-start | bytes 2097152 | tf_op jit(solution)/shard_map/all_to_all | solution.py:60
  111.7 55.7 %all-to-all-start.4 = ((f32[8,8,512]{2,0,1:T(8,128)}), f32[8,8,512]{2,0,1:T(8,128)S(1)}, u32[]{:S(2)}, u32[]{:S(2)}) async-start(f32[8,8,512]{2,0,1:T(8,128)} %fusion.6), calls=%async_computation.4 | async-start | bytes 262144 | tf_op jit(solution)/shard_map/all_to_all | solution.py:73
